TPU v7x, 32 devices: a whole 2x2x4 slice. The times are simulated.
32 devices in a mesh: parts: 2 (over x), seq: 16 (over z, y, core).
Axes of the slice: x: 2, y: 2, z: 4, core: 2. Of those that a mesh axis runs over, the one named last changes fastest.
Arguments:
- token_ids: int32 [4, 4], P(None, 'parts'), parts along dimension 1, may hold values from 0 to 76031
- lengths: int32 [4], P('parts'), parts along dimension 0, may hold values from 24576 to 32768, as said below
- embed_table: bfloat16 [76032, 5120], P('seq'), may hold values from -6 to 6
- attn_gain: bfloat16 [5120], replicated, may hold values from 0.25 to 1.75
- w_qkv: bfloat16 [5120, 7168], P('seq'), may hold values from -0.125 to 0.125
- qkv_bias: float32 [7168], replicated, may hold values from -8 to 8
- cache_keys: bfloat16 [4, 32768, 1024], P('parts', 'seq'), parts along dimension 0, may hold values from -300 to 300
- cache_values: bfloat16 [4, 32768, 1024], P('parts', 'seq'), parts along dimension 0, may hold values from -6 to 6
- w_out: bfloat16 [5120, 5120], P(None, 'seq'), may hold values from -0.078125 to 0.078125
- mlp_gain: bfloat16 [5120], replicated, may hold values from 0.25 to 1.75
- w_gate: bfloat16 [5120, 16384], P(None, 'seq'), may hold values from -0.078125 to 0.078125
- w_up: bfloat16 [5120, 16384], P(None, 'seq'), may hold values from -0.078125 to 0.078125
- w_down: bfloat16 [16384, 5120], P('seq'), may hold values from -0.0625 to 0.0625
Outputs:
- attended: bfloat16 [4, 4, 5120], P(None, 'parts'), parts along dimension 1
- layer_out: bfloat16 [4, 4, 5120], P(None, 'parts', 'seq'), parts along dimension 1
There are 2 independent parts, one for each index of `parts`. A program takes and returns all parts, laid end to end along the dimension named above; an argument that names none is the same for every part. Nothing has to cross between parts.
Inputs may be any that keep to these rules, and one draw needn't show every extreme that they name: Cache positions lengths[b] and later are unused; the first prompt fills the whole cache of 32768 positions.
All inputs are finite; a program needn't handle non-finite values.
Results may differ from a plain program's by a relative error of at most 0.017.
The roundings to bfloat16 on the way count: a program that leaves them out, or rounds other values in their place, can miss the bound.
Values may be sent and summed in bfloat16 or wider, within the bound.
A program may use at most 192 MiB of HBM per device.

v0:
```python
import functools
import math

import jax
import jax.numpy as jnp
from jax import lax
from jax.experimental import pallas as pl
from jax.experimental.pallas import tpu as pltpu
from jax.sharding import PartitionSpec as P

HEADS = 40
KV_HEADS = 8
HEAD_DIM = 128

NORM_EPS = 1e-06
ROPE_BASE = 1000000.0
MASKED = -1e30
F32 = jnp.float32
BF16 = jnp.bfloat16
MESH = pl.DeviceIdType.MESH


def layer_kernel(
    n,
    lengths,
    picked,
    inside,
    gain_one,
    bias,
    cos,
    sin,
    gain_two,
    qkv_hbm,
    keys_hbm,
    values_hbm,
    out_hbm,
    gate_hbm,
    up_hbm,
    down_hbm,
    attended_ref,
    layer_ref,
    w_qkv,
    keys,
    values,
    w_out,
    w_gate,
    w_up,
    w_down,
    rows_out,
    rows_in,
    joint_out,
    joint_in,
    heads_all,
    heads_wide,
    part_out,
    part_in,
    attended_all,
    mid_all,
    wide,
    narrow,
    down_out,
    down_in,
    group_sum,
    group_top,
    group_total,
    load_sem,
    send_sem,
    recv_sem,
):
    me = lax.axis_index("seq")
    group = HEADS // KV_HEADS
    joint_heads = HEADS + 2 * KV_HEADS
    tokens, width = picked.shape
    batches = keys.shape[0]
    local_len = keys.shape[1]
    cols = w_out.shape[0]
    joint_each = joint_out.shape[1]
    head_each = part_out.shape[1] - 1
    scale = 1.0 / math.sqrt(HEAD_DIM)

    loads = [
        pltpu.make_async_copy(a, b, load_sem.at[i])
        for i, (a, b) in enumerate(
            (
                (qkv_hbm, w_qkv),
                (keys_hbm, keys),
                (values_hbm, values),
                (out_hbm, w_out),
                (gate_hbm, w_gate),
                (up_hbm, w_up),
                (down_hbm, w_down),
            )
        )
    ]
    for load in loads:
        load.start()

    barrier = pltpu.get_barrier_semaphore()

    @pl.loop(1, n)
    def _(d):
        pl.semaphore_signal(
            barrier, inc=1, device_id={"seq": lax.rem(me + d, n)}, device_id_type=MESH
        )

    def copy_to(step, source, target, slot, peer):
        return pltpu.make_async_remote_copy(
            src_ref=source,
            dst_ref=target.at[slot],
            send_sem=send_sem.at[step, peer],
            recv_sem=recv_sem.at[step, slot],
            device_id={"seq": peer},
            device_id_type=MESH,
        )

    def send_all(step, source, target, spread):
        @pl.loop(1, n)
        def _(d):
            peer = lax.rem(me + d, n)
            copy_to(step, source.at[peer if spread else me], target, me, peer).start()

    def receive_all(step, target):
        @pl.loop(1, n)
        def _(d):
            peer = lax.rem(me + d, n)
            copy_to(step, target.at[peer], target, peer, peer).wait_recv()

    def sent_all(step, source, spread):
        @pl.loop(1, n)
        def _(d):
            peer = lax.rem(me + d, n)
            src = source.at[peer if spread else me]
            pltpu.make_async_remote_copy(
                src_ref=src,
                dst_ref=src,
                send_sem=send_sem.at[step, peer],
                recv_sem=recv_sem.at[step, peer],
                device_id={"seq": peer},
                device_id_type=MESH,
            ).wait_send()

    wide[...] = picked[...].astype(F32) * inside[...]
    mean_square = jnp.sum(wide[...] * wide[...], axis=1, keepdims=True) / width
    normed = (wide[...] * lax.rsqrt(mean_square + NORM_EPS) * gain_one[...].astype(F32)[None, :]).astype(BF16)
    heads_out = jnp.concatenate([wide[...], normed.astype(F32)], axis=0)
    for j in range(n):
        rows_out[j] = heads_out[:, j * cols : (j + 1) * cols].astype(BF16)
    part_out[...] = jnp.zeros_like(part_out)
    pl.semaphore_wait(barrier, n - 1)
    send_all(0, rows_out, rows_in, True)
    rows_in[me] = rows_out[me]
    receive_all(0, rows_in)
    rows = lax.fori_loop(
        1, n, lambda j, acc: acc + rows_in[j].astype(F32), rows_in[0].astype(F32)
    )
    stream = rows[:tokens]
    normed_local = rows[tokens:].astype(BF16)

    loads[0].wait()
    chunk = 4

    @pl.loop(0, joint_heads // chunk, unroll=True)
    def _(c):
        part = jnp.dot(
            normed_local,
            w_qkv[:, pl.ds(pl.multiple_of(c * (chunk * HEAD_DIM), HEAD_DIM), chunk * HEAD_DIM)],
            preferred_element_type=F32,
        )
        for i in range(chunk):
            h = c * chunk + i
            joint_out[h // joint_each, h % joint_each] = part[:, i * HEAD_DIM : (i + 1) * HEAD_DIM]

    for h in range(joint_heads, n * joint_each):
        joint_out[h // joint_each, h % joint_each] = jnp.zeros((tokens, HEAD_DIM), F32)
    send_all(1, joint_out, joint_in, True)
    joint_in[me] = joint_out[me]
    receive_all(1, joint_in)
    joint = lax.fori_loop(1, n, lambda j, acc: acc + joint_in[j], joint_in[0])
    tiles = []
    for i in range(joint_each):
        h = jnp.minimum(me * joint_each + i, joint_heads - 1)
        x = (joint[i] + bias[pl.ds(h, 1), :]).astype(BF16).astype(F32)
        turned = x * cos[...] + pltpu.roll(x, HEAD_DIM // 2, 1) * sin[...]
        is_key = jnp.full(x.shape, h, jnp.int32) < HEADS + KV_HEADS
        tiles.append(jnp.where(is_key, turned, x))
    heads_all[me] = jnp.concatenate(tiles, axis=0).astype(BF16)
    send_all(2, heads_all, heads_all, False)
    receive_all(2, heads_all)
    rows_each = joint_each * tokens

    @pl.loop(0, n)
    def _(j):
        heads_wide[pl.ds(pl.multiple_of(j * rows_each, 8), rows_each), :] = heads_all[j].astype(F32)

    loads[1].wait()
    loads[2].wait()
    group_rows = group * tokens
    places = me * local_len + lax.broadcasted_iota(jnp.int32, (1, local_len), 1)
    lane = lax.broadcasted_iota(jnp.int32, (tokens, HEAD_DIM), 1)

    exponent = scale / math.log(2.0)

    @pl.loop(0, KV_HEADS)
    def _(k):
        head_cols = pl.ds(pl.multiple_of(k * HEAD_DIM, HEAD_DIM), HEAD_DIM)
        half = group_rows // batches
        for b in range(batches):
            own_rows = pl.ds(b, half, stride=batches)
            q = heads_wide[pl.ds(k * group_rows + b, half, stride=batches), :].astype(BF16)
            scores = lax.dot_general(
                q, keys[b, :, head_cols], (((1,), (1,)), ((), ())), preferred_element_type=F32
            )
            masked = jnp.where(places < lengths[b], scores, MASKED)
            own_top = jnp.max(masked, axis=1, keepdims=True)
            weight = jnp.exp2((masked - own_top) * exponent)
            own_total = jnp.sum(weight, axis=1, keepdims=True)
            own_sum = jnp.dot(
                weight.astype(BF16), values[b, :, head_cols], preferred_element_type=F32
            )
            group_sum[own_rows, :] = own_sum
            group_top[own_rows, :] = jnp.broadcast_to(own_top * scale, own_sum.shape)
            group_total[own_rows, :] = jnp.broadcast_to(own_total, own_sum.shape)
        summed, top, total = group_sum[...], group_top[...], group_total[...]
        for g in range(group):
            h = k * group + g
            owner, slot = h // head_each, h % head_each
            mine = slice(g * tokens, (g + 1) * tokens)
            part_out[owner, slot] = summed[mine]
            stats = part_out[owner, head_each]
            stats = jnp.where(lane == 2 * slot, top[mine], stats)
            part_out[owner, head_each] = jnp.where(lane == 2 * slot + 1, total[mine], stats)

    send_all(3, part_out, part_in, True)
    part_in[me] = part_out[me]

    row = lax.broadcasted_iota(jnp.int32, (tokens, 1), 0)
    fresh = []
    for i in range(head_each):
        h = jnp.minimum(me * head_each + i, HEADS - 1)
        kv = h // group
        q = heads_wide[pl.ds(pl.multiple_of(h * tokens, 8), tokens), :]
        new_key = heads_wide[pl.ds(pl.multiple_of((HEADS + kv) * tokens, 8), tokens), :]
        new_value = heads_wide[
            pl.ds(pl.multiple_of((HEADS + KV_HEADS + kv) * tokens, 8), tokens), :
        ]
        scores = []
        top = jnp.full((tokens, 1), MASKED, F32)
        for t in range(tokens):
            seen = (row % batches == t % batches) & (row >= t)
            score = jnp.sum(q * new_key[t : t + 1], axis=1, keepdims=True) * scale
            score = jnp.where(seen, score, MASKED)
            scores.append((seen, score))
            top = jnp.maximum(top, score)
        fresh.append((top, scores, new_value))

    receive_all(3, part_in)
    tiles = []
    for i in range(head_each):
        top, scores, new_value = fresh[i]

        def stat(j, which):
            return jnp.broadcast_to(
                part_in[j, head_each][:, 2 * i + which : 2 * i + which + 1], (tokens, HEAD_DIM)
            )

        top = jnp.broadcast_to(top, (tokens, HEAD_DIM))
        top = lax.fori_loop(0, n, lambda j, m: jnp.maximum(m, stat(j, 0)), top, unroll=True)
        total = jnp.zeros((tokens, HEAD_DIM), F32)
        summed = jnp.zeros((tokens, HEAD_DIM), F32)
        for t in range(tokens):
            seen, score = scores[t]
            weight = jnp.where(seen, jnp.exp(score - top), 0.0)
            total += weight
            summed += weight.astype(BF16).astype(F32) * new_value[t : t + 1]

        def merge(j, state):
            total, summed = state
            factor = jnp.exp(stat(j, 0) - top)
            return total + stat(j, 1) * factor, summed + part_in[j, i] * factor

        total, summed = lax.fori_loop(0, n, merge, (total, summed), unroll=True)
        tiles.append(summed / total)
    attended_all[me] = jnp.concatenate(tiles, axis=0).astype(BF16)
    send_all(4, attended_all, attended_all, False)
    receive_all(4, attended_all)
    for h in range(HEADS):
        at = (h % head_each) * tokens
        wide[:, h * HEAD_DIM : (h + 1) * HEAD_DIM] = attended_all[h // head_each].astype(F32)[
            at : at + tokens
        ]
    narrow[...] = wide[...].astype(BF16)
    attended_ref[...] = narrow[...]

    loads[3].wait()
    depth = 512

    def piece(c):
        return pl.ds(pl.multiple_of(c * depth, depth), depth)

    mid = stream + lax.fori_loop(
        0,
        width // depth,
        lambda c, acc: acc
        + lax.dot_general(
            narrow[:, piece(c)],
            w_out[:, piece(c)],
            (((1,), (1,)), ((), ())),
            preferred_element_type=F32,
        ),
        jnp.zeros((tokens, cols), F32),
        unroll=True,
    )
    mid_all[me] = mid
    send_all(5, mid_all, mid_all, False)
    receive_all(5, mid_all)
    for j in range(n):
        wide[:, j * cols : (j + 1) * cols] = mid_all[j]
    mean_square = jnp.sum(wide[...] * wide[...], axis=1, keepdims=True) / width
    narrow[...] = (wide[...] * lax.rsqrt(mean_square + NORM_EPS) * gain_two[...].astype(F32)[None, :]).astype(BF16)

    loads[4].wait()
    loads[5].wait()
    units = w_gate.shape[1]

    def both(c, state):
        gate, upper = state
        x = narrow[:, piece(c)]
        return (
            gate + jnp.dot(x, w_gate[piece(c), :], preferred_element_type=F32),
            upper + jnp.dot(x, w_up[piece(c), :], preferred_element_type=F32),
        )

    zero = jnp.zeros((tokens, units), F32)
    gate, upper = lax.fori_loop(0, width // depth, both, (zero, zero), unroll=True)
    hidden = (gate / (1.0 + jnp.exp(-gate)) * upper).astype(BF16)
    loads[6].wait()

    @pl.loop(0, width // depth, unroll=True)
    def _(c):
        wide[:, piece(c)] = jnp.dot(hidden, w_down[:, piece(c)], preferred_element_type=F32)

    for j in range(n):
        down_out[j] = wide[:, j * cols : (j + 1) * cols]
    send_all(6, down_out, down_in, True)
    down_in[me] = down_out[me]
    receive_all(6, down_in)
    summed = lax.fori_loop(1, n, lambda j, acc: acc + down_in[j], down_in[0])
    layer_ref[...] = (mid + summed).astype(BF16)

    sent_all(0, rows_out, True)
    sent_all(1, joint_out, True)
    sent_all(2, heads_all, False)
    sent_all(3, part_out, True)
    sent_all(4, attended_all, False)
    sent_all(5, mid_all, False)
    sent_all(6, down_out, True)


def body(
    token_ids,
    lengths,
    embed_table,
    attn_gain,
    w_qkv,
    qkv_bias,
    cache_keys,
    cache_values,
    w_out,
    mlp_gain,
    w_gate,
    w_up,
    w_down,
):
    n = lax.axis_size("seq")
    rank = lax.axis_index("seq")
    step_count, batch_count = token_ids.shape
    tokens = step_count * batch_count
    width = embed_table.shape[1]
    vocab_rows = embed_table.shape[0]
    cols = w_out.shape[1]
    local_ids = token_ids.reshape(-1) - rank * vocab_rows
    inside = (local_ids >= 0) & (local_ids < vocab_rows)
    picked = embed_table.at[jnp.clip(local_ids, 0, vocab_rows - 1)].get(mode="promise_in_bounds")
    positions = (lengths[None, :] + jnp.arange(step_count, dtype=jnp.int32)[:, None]).reshape(-1)
    half = HEAD_DIM // 2
    frequency = ROPE_BASE ** (-2.0 * jnp.arange(half, dtype=F32) / HEAD_DIM)
    angles = positions.astype(F32)[:, None] * frequency
    cosine, sine = jnp.cos(angles), jnp.sin(angles)
    cos = jnp.concatenate([cosine, cosine], axis=1)
    sin = jnp.concatenate([-sine, sine], axis=1)
    joint_heads = HEADS + 2 * KV_HEADS
    joint_each = -(-joint_heads // n)
    head_each = -(-HEADS // n)
    vmem = pl.BlockSpec(memory_space=pltpu.VMEM)
    hbm = pl.BlockSpec(memory_space=pl.ANY)
    attended, layer_out = pl.pallas_call(
        functools.partial(layer_kernel, n),
        out_shape=(
            jax.ShapeDtypeStruct((tokens, width), BF16),
            jax.ShapeDtypeStruct((tokens, cols), BF16),
        ),
        in_specs=[pl.BlockSpec(memory_space=pltpu.SMEM)] + [vmem] * 7 + [hbm] * 7,
        out_specs=(vmem, vmem),
        scratch_shapes=[
            pltpu.VMEM(a.shape, a.dtype)
            for a in (w_qkv, cache_keys, cache_values, w_out.T, w_gate, w_up, w_down)
        ]
        + [
            pltpu.VMEM((n, 2 * tokens, cols), BF16),
            pltpu.VMEM((n, 2 * tokens, cols), BF16),
            pltpu.VMEM((n, joint_each, tokens, HEAD_DIM), F32),
            pltpu.VMEM((n, joint_each, tokens, HEAD_DIM), F32),
            pltpu.VMEM((n, joint_each * tokens, HEAD_DIM), BF16),
            pltpu.VMEM((n * joint_each * tokens, HEAD_DIM), F32),
            pltpu.VMEM((n, head_each + 1, tokens, HEAD_DIM), F32),
            pltpu.VMEM((n, head_each + 1, tokens, HEAD_DIM), F32),
            pltpu.VMEM((n, head_each * tokens, HEAD_DIM), BF16),
            pltpu.VMEM((n, tokens, cols), F32),
            pltpu.VMEM((tokens, width), F32),
            pltpu.VMEM((tokens, width), BF16),
            pltpu.VMEM((n, tokens, cols), F32),
            pltpu.VMEM((n, tokens, cols), F32),
            pltpu.VMEM((HEADS // KV_HEADS * tokens, HEAD_DIM), F32),
            pltpu.VMEM((HEADS // KV_HEADS * tokens, HEAD_DIM), F32),
            pltpu.VMEM((HEADS // KV_HEADS * tokens, HEAD_DIM), F32),
            pltpu.SemaphoreType.DMA((7,)),
            pltpu.SemaphoreType.DMA((7, n)),
            pltpu.SemaphoreType.DMA((7, n)),
        ],
        compiler_params=pltpu.CompilerParams(
            collective_id=0, has_side_effects=True, vmem_limit_bytes=67043328
        ),
    )(
        lengths,
        picked,
        inside.astype(F32)[:, None],
        attn_gain,
        qkv_bias.reshape(joint_heads, HEAD_DIM),
        cos,
        sin,
        mlp_gain,
        w_qkv,
        cache_keys,
        cache_values,
        w_out.T,
        w_gate,
        w_up,
        w_down,
    )
    return (
        attended.reshape(step_count, batch_count, width),
        layer_out.reshape(step_count, batch_count, cols),
    )


def solution(mesh):
    return jax.shard_map(
        body,
        mesh=mesh,
        in_specs=(
            P(None, "parts"),
            P("parts"),
            P("seq", None),
            P(),
            P("seq", None),
            P(),
            P("parts", "seq", None),
            P("parts", "seq", None),
            P(None, "seq"),
            P(),
            P(None, "seq"),
            P(None, "seq"),
            P("seq", None),
        ),
        out_specs=(P(None, "parts", None), P(None, "parts", "seq")),
        check_vma=False,
    )
```

profile of v0, /device:TPU:0, one launch (start us, length us, event | category | flops | bytes accessed | tf_op | source)
XLA Modules:
  0.0 78.3 jit_solution(10684319306363817651)
XLA Ops:
  0.6 0.7 and_convert_fusion
  1.3 0.7 subtract_clamp_fusion
  2.0 0.1 copy.18
  2.1 0.1 min.12
  2.2 0.1 copy.19
  2.3 0.7 reshape.97.inside
  3.0 0.7 add_convert_fusion
  3.6 0.1 convert_element_type.26
  3.7 0.1 fusion
  3.8 0.7 pad_maximum_fusion
  4.5 2.5 %gather_fusion = bf16[8,5120]{1,0:T(8,128)(2,1)} fusion(bf16[4752,5120]{1,0:T(8,128)(2,1)} %param.15, s32[1024]{0:T(1024)S(1)} %pad_clamp_fusion), kind=kCustom, calls=%fused_computation | custom fusion | bytes 163872 | tf_op jit(solution)/shard_map/gather | solution.py:383
  7.0 68.4 %shard_map.140 = (bf16[8,5120]{1,0:T(8,128)(2,1)}, bf16[8,320]{1,0:T(8,128)(2,1)}) custom-call(s32[2]{0:T(128)} %lengths.1, bf16[8,5120]{1,0:T(8,128)(2,1)} %gather_fusion, f32[8,1]{1,0:T(8,128)} %reshape.97.inside, bf16[5120]{0:T(1024)(128)(2,1)} %gain_one.1, f32[56,128]{1,0:T(8,128)} %bitcast.5, f32[8,128]{1,0:T(8,128)} %get-tuple-element.9.cos, ...), custom_call_target="tpu_custom_call" | custom-call | tf_op jit(solution)/shard_map/pallas_call | solution.py:396
  75.5 1.6 %reshape.86 = bf16[4,2,5120]{2,1,0:T(2,128)(2,1)} reshape(bf16[8,5120]{1,0:T(8,128)(2,1)} %get-tuple-element.4) | data formatting | bytes 163840 | tf_op jit(solution)/shard_map/reshape | solution.py:451
  77.0 1.3 %reshape.87 = bf16[4,2,320]{2,1,0:T(2,128)(2,1)} reshape(bf16[8,320]{1,0:T(8,128)(2,1)} %get-tuple-element.5) | data formatting | bytes 10240 | tf_op jit(solution)/shard_map/reshape | solution.py:452
  (3 shorter events, 0.0 us)
where the time goes:
time: 78.7 us; the launch traced here: 78.3 us
  Pallas kernels  68.4 us (87%)
  local copies, waits for them, and re-layouts  6.37 us (8%)
  other arithmetic  2.84 us (4%)
    pallas_call x1, Pallas kernels, body(): pl.pallas_call(functools.partial(layer_kernel, n), out_shape=(jax.ShapeDt...  68.4 us
    gather x1, local copies, waits for them, and re-layouts, body(): embed_table.at[jnp.clip(local_ids, 0, vocab_rows - 1)]  2.49 us

commit v1 on v0

v1 whole, which is shorter than its diff:
```python
import functools
import math

import jax
import jax.numpy as jnp
import numpy as np
from jax import lax
from jax.experimental import pallas as pl
from jax.experimental.pallas import tpu as pltpu
from jax.sharding import PartitionSpec as P

HEADS = 40
KV_HEADS = 8
HEAD_DIM = 128
GROUP = HEADS // KV_HEADS
LOCAL = GROUP + 2
LANES = 128

NORM_EPS = 1e-06
ROPE_BASE = 1000000.0
MASKED = -1e30
F32 = jnp.float32
BF16 = jnp.bfloat16
MESH = pl.DeviceIdType.MESH

FIRST_RECEIVE = (0, 1, 2, 2 + KV_HEADS, 3 + KV_HEADS, 3 + 2 * KV_HEADS, 11 + 2 * KV_HEADS)
RECEIVES = 12 + 2 * KV_HEADS


def pieces_of(value, count):
    out = []
    for _ in range(count):
        piece = value.astype(BF16).astype(F32)
        out.append(piece)
        value = value - piece
    return out


def gather_kernel(
    n,
    ids_hbm,
    lengths_hbm,
    gain_one_hbm,
    gain_two_hbm,
    table,
    blocks,
    gains,
    misc,
    ids,
    lengths,
    gain_one,
    gain_two,
    rows,
    wide,
    sem,
    row_sem,
):
    me = lax.axis_index("seq")
    small = [
        pltpu.make_async_copy(a, b, sem.at[i])
        for i, (a, b) in enumerate(
            (
                (ids_hbm, ids),
                (lengths_hbm, lengths),
                (gain_one_hbm, gain_one),
                (gain_two_hbm, gain_two),
            )
        )
    ]
    for copy in small:
        copy.start()
    first = lax.broadcasted_iota(jnp.int32, (1, LANES), 1)
    half = HEAD_DIM // 2
    frequency = jnp.zeros((1, LANES), F32)
    for i in range(half):
        value = float(np.float32(ROPE_BASE ** (-2.0 * i / HEAD_DIM)))
        frequency = jnp.where(first % half == i, value, frequency)
    batches, steps = ids.shape
    small[0].wait()
    tokens = batches * steps
    vocab_rows, width = table.shape
    cols = width // n
    row = lax.broadcasted_iota(jnp.int32, (tokens, tokens * 8), 0)
    lane = lax.broadcasted_iota(jnp.int32, (tokens, tokens * 8), 1)
    target = jnp.full((tokens, tokens * 8), -1, jnp.int32)
    copies = []
    for t in range(tokens):
        local = ids[t // steps, t % steps] - me * vocab_rows
        inside = (local >= 0) & (local < vocab_rows)
        local = jnp.clip(local, 0, vocab_rows - 1)
        base = local // 8
        copy = pltpu.make_async_copy(
            table.at[pl.ds(pl.multiple_of(base * 8, 8), 8), :], rows.at[t], row_sem.at[t]
        )
        copy.start()
        copies.append(copy)
        target = jnp.where(row == t, jnp.where(inside, t * 8 + local - base * 8, -1), target)
    one_hot = jnp.where(lane == target, 1.0, 0.0).astype(BF16)

    for copy in small[1:]:
        copy.wait()
    for j in range(n):
        own = slice(j * cols, (j + 1) * cols)
        gains[j, 0:1, :] = gain_one[...].astype(F32)[None, own]
        gains[j, 1:2, :] = gain_two[...].astype(F32)[None, own]
    token = lax.broadcasted_iota(jnp.int32, (tokens, LANES), 0)
    place = jnp.zeros((tokens, LANES), jnp.int32)
    for b in range(batches):
        place = jnp.where(token // steps == b, lengths[b] + token % steps, place)
        misc[2, b : b + 1, :] = jnp.full((1, LANES), lengths[b], jnp.int32).astype(F32)
    angle = place.astype(F32) * frequency
    sine = jnp.sin(angle)
    first = lax.broadcasted_iota(jnp.int32, (tokens, LANES), 1) < HEAD_DIM // 2
    misc[0] = jnp.cos(angle)
    misc[1] = jnp.where(first, -sine, sine)

    for copy in copies:
        copy.wait()
    found = rows[...].astype(F32).reshape(tokens * 8, width).astype(BF16)
    wide[...] = jnp.dot(one_hot, found, preferred_element_type=F32)
    square = jnp.sum(wide[...] * wide[...], axis=1, keepdims=True)
    spare = blocks.shape[2] - cols
    at = lax.broadcasted_iota(jnp.int32, (tokens, spare), 1)
    extra = jnp.zeros((tokens, spare), F32)
    for i, piece in enumerate(pieces_of(square, 3)):
        extra = jnp.where(at == i, piece, extra)
    extra = extra.astype(BF16)
    for j in range(n):
        blocks[j, :, :cols] = wide[:, j * cols : (j + 1) * cols].astype(BF16)
        blocks[j, :, cols:] = extra


def layer_kernel(
    n,
    blocks,
    gains,
    misc,
    bias_hbm,
    qkv_hbm,
    keys_hbm,
    values_hbm,
    out_hbm,
    gate_hbm,
    up_hbm,
    down_hbm,
    attended_ref,
    layer_ref,
    bias,
    w_qkv,
    keys,
    values,
    w_out,
    w_gate,
    w_up,
    w_down,
    rows_in,
    joint_out,
    joint_in,
    heads_all,
    own_heads,
    part_out,
    part_in,
    fresh,
    spread,
    attended_all,
    mid_all,
    wide,
    down_out,
    down_in,
    load_sem,
    send_sem,
    recv_sem,
):
    me = lax.axis_index("seq")
    tokens = blocks.shape[1]
    block_width = blocks.shape[2]
    batches, local_len = keys.shape[0], keys.shape[1]
    steps = tokens // batches
    cols, width = w_out.shape
    units = w_gate.shape[1]
    pairs = KV_HEADS // 2
    group_width = GROUP * HEAD_DIM
    scale = 1.0 / math.sqrt(HEAD_DIM)
    first_owner = n // 2 - KV_HEADS // 2
    is_owner = (me >= first_owner) & (me < first_owner + KV_HEADS)
    mine = jnp.clip(me - first_owner, 0, KV_HEADS - 1)
    side = me // (n // 2)
    turn = (me // 2) % 2

    loads = [
        pltpu.make_async_copy(a, b, load_sem.at[i])
        for i, (a, b) in enumerate(
            (
                (qkv_hbm, w_qkv),
                (bias_hbm, bias),
                (keys_hbm, keys),
                (values_hbm, values),
                (out_hbm, w_out),
                (gate_hbm, w_gate),
                (up_hbm, w_up),
                (down_hbm, w_down),
            )
        )
    ]
    barrier = pltpu.get_barrier_semaphore()

    @pl.loop(1, n)
    def _(d):
        pl.semaphore_signal(
            barrier, inc=1, device_id={"seq": lax.rem(me + d, n)}, device_id_type=MESH
        )

    for load in loads:
        load.start()

    unrolled = n & (n - 1) == 0 and n <= 32
    staged = unrolled and n // 4 <= 6 and cols % 16 == 0 and (4 * cols) % LANES == 0
    bits = n.bit_length() - 1
    flips = [(1 << k) * (1 - 2 * ((me // (1 << k)) % 2)) for k in range(bits)]

    def partner(d):
        return me + sum(flips[k] for k in range(bits) if d >> k & 1)

    def arrival_of(d):
        return 0 if d == 1 else 1 if d < 4 else 1 + d // 4

    def each_peer(act):
        if unrolled:
            for d in range(n - 1, 0, -1):
                act(partner(d))
        else:

            @pl.loop(1, n)
            def _(d):
                act(lax.rem(me + d, n))

    def copy_to(step, source, target, slot, peer, arrival=0):
        return pltpu.make_async_remote_copy(
            src_ref=source,
            dst_ref=target.at[slot],
            send_sem=send_sem.at[step],
            recv_sem=recv_sem.at[FIRST_RECEIVE[step] + arrival],
            device_id={"seq": peer},
            device_id_type=MESH,
        )

    def of_bytes(step, whole, arrival=0):
        return pltpu.make_async_remote_copy(
            src_ref=whole,
            dst_ref=whole,
            send_sem=send_sem.at[step],
            recv_sem=recv_sem.at[FIRST_RECEIVE[step] + arrival],
            device_id={"seq": lax.rem(me + 1, n)},
            device_id_type=MESH,
        )

    def landed(step, whole, arrival=0):
        of_bytes(step, whole, arrival).wait_recv()

    def departed(step, whole):
        of_bytes(step, whole).wait_send()

    def departed_to_owners(step, target):
        @pl.when(is_owner)
        def _():
            departed(step, target.at[pl.ds(0, KV_HEADS - 1)])

        @pl.when(jnp.logical_not(is_owner))
        def _():
            departed(step, target.at[pl.ds(0, KV_HEADS)])

    others = pl.ds(0, n - 1)

    def interleaved(s, count):
        picked = [wide[b * steps + s : b * steps + s + 1, :count] for b in range(batches)]
        return jnp.concatenate(picked, axis=0).astype(BF16)

    row = lax.broadcasted_iota(jnp.int32, (1, tokens, LANES), 1)
    upper = row < steps
    lane = lax.broadcasted_iota(jnp.int32, (tokens, LANES), 1)

    pl.semaphore_wait(barrier, n - 1)
    each_peer(lambda peer: copy_to(0, blocks.at[peer], rows_in, me, peer).start())
    rows_in[me] = blocks[me]
    for g in range(GROUP):
        at = lax.broadcasted_iota(jnp.int32, (LANES, LANES), 0)
        spread[:, g * LANES : (g + 1) * LANES] = jnp.where(
            (at >= g * 8) & (at < g * 8 + 3), 1.0, 0.0
        ).astype(BF16)
        spread[:, (GROUP + g) * LANES : (GROUP + g + 1) * LANES] = jnp.where(
            (at >= g * 8 + 3) & (at < g * 8 + 6), 1.0, 0.0
        ).astype(BF16)
    landed(0, rows_in.at[others])
    rows = rows_in[0].astype(F32)
    for j in range(1, n):
        rows += rows_in[j].astype(F32)
    stream = rows[:, :cols]
    square = jnp.sum(rows[:, cols : cols + 3], axis=1, keepdims=True)
    gain = gains[me]
    normed = (stream * lax.rsqrt(square / width + NORM_EPS) * gain[0:1]).astype(BF16)

    loads[0].wait()
    loads[1].wait()
    for i in range(pairs):
        c = side * i + (1 - side) * (pairs - 1 - i)
        q_part = jnp.dot(
            normed,
            w_qkv[:, pl.ds(pl.multiple_of(c * 2 * group_width, LANES), 2 * group_width)],
            preferred_element_type=F32,
        )
        k_part = jnp.dot(
            normed,
            w_qkv[:, pl.ds(pl.multiple_of((HEADS + 2 * c) * LANES, LANES), 2 * LANES)],
            preferred_element_type=F32,
        )
        v_part = jnp.dot(
            normed,
            w_qkv[:, pl.ds(pl.multiple_of((HEADS + KV_HEADS + 2 * c) * LANES, LANES), 2 * LANES)],
            preferred_element_type=F32,
        )
        for p in range(2):
            k = 2 * c + p
            owner = first_owner + k
            for g in range(GROUP):
                at = p * group_width + g * LANES
                joint_out[k, g] = q_part[:, at : at + LANES].astype(BF16)
            joint_out[k, GROUP] = k_part[:, p * LANES : (p + 1) * LANES].astype(BF16)
            joint_out[k, GROUP + 1] = v_part[:, p * LANES : (p + 1) * LANES].astype(BF16)

            @pl.when(owner != me)
            def _():
                copy_to(1, joint_out.at[k], joint_in, me, owner).start()

    departed(0, rows_in.at[others])

    @pl.when(is_owner)
    def _():
        joint_in[me] = joint_out[mine]
        landed(1, joint_in.at[others])
        joint = joint_in[0].astype(F32)
        for j in range(1, n):
            joint += joint_in[j].astype(F32)
        odd = mine % 2
        swap = jnp.full((tokens, LANES), odd, jnp.int32) == 1
        cos, sin = misc[0], misc[1]

        def biased(i, h):
            return (joint[i] + bias[pl.ds(h, 1), :]).astype(BF16).astype(F32)

        def turned(x):
            x = x * cos + pltpu.roll(x, HEAD_DIM // 2, 1) * sin
            return x.astype(BF16).astype(F32)

        for g in range(GROUP):
            x = turned(biased(g, mine * GROUP + g))
            x = jnp.where(swap, pltpu.roll(x, steps, 0), x)
            own_heads[g] = x
            heads_all[mine, g] = x.astype(BF16)
        each_peer(lambda peer: copy_to(2, heads_all.at[mine], heads_all, mine, peer, mine).start())
        own_heads[GROUP] = turned(biased(GROUP, HEADS + mine))
        own_heads[GROUP + 1] = biased(GROUP + 1, HEADS + KV_HEADS + mine)

        q = own_heads[:GROUP].reshape(GROUP * tokens, HEAD_DIM).astype(BF16)
        new_keys = own_heads[GROUP].astype(BF16)
        new_values = own_heads[GROUP + 1].astype(BF16)
        shape = (GROUP * tokens, tokens)
        at = lax.broadcasted_iota(jnp.int32, shape, 0) % tokens
        other = lax.broadcasted_iota(jnp.int32, shape, 1)
        prompt = (at // steps + odd) % 2
        seen = (other // steps == prompt) & (other % steps <= at % steps)
        score = lax.dot_general(q, new_keys, (((1,), (1,)), ((), ())), preferred_element_type=F32)
        score = jnp.where(seen, score * scale, MASKED)
        top = jnp.max(score, axis=1, keepdims=True)
        weight = jnp.where(seen, jnp.exp(score - top), 0.0)
        total = jnp.sum(weight, axis=1, keepdims=True)
        summed = jnp.dot(weight.astype(BF16), new_values, preferred_element_type=F32)
        wide_shape = (GROUP, tokens, LANES)
        fresh[0] = summed.reshape(wide_shape)
        fresh[1] = jnp.broadcast_to(top, (GROUP * tokens, LANES)).reshape(wide_shape)
        fresh[2] = jnp.broadcast_to(total, (GROUP * tokens, LANES)).reshape(wide_shape)

    departed_to_owners(1, joint_out)

    loads[2].wait()
    loads[3].wait()
    places = (
        me * local_len + lax.broadcasted_iota(jnp.int32, (1, local_len), 1)
    ).astype(F32)
    exponent = scale / math.log(2.0)
    order = [
        2 * side + turn,
        2 * side + 1 - turn,
        2 * (1 - side) + turn,
        2 * (1 - side) + 1 - turn,
    ]
    for near in range(2):
        for c in order[2 * near : 2 * near + 2]:
            for p in range(2):
                k = 2 * c + p

                @pl.when(first_owner + k != me)
                def _():
                    landed(2, heads_all.at[k], k)

        for c in order[2 * near : 2 * near + 2]:
            first = heads_all[2 * c].astype(F32)
            second = heads_all[2 * c + 1].astype(F32)
            pair_cols = pl.ds(pl.multiple_of(c * 2 * HEAD_DIM, LANES), 2 * HEAD_DIM)
            sums, tops, totals = [], [], []
            for b in range(batches):
                chosen = upper if b == 0 else ~upper
                q = jnp.concatenate(
                    [jnp.where(chosen, first, 0.0), jnp.where(chosen, 0.0, second)], axis=2
                )
                q = q.reshape(GROUP * tokens, 2 * HEAD_DIM).astype(BF16)
                scores = lax.dot_general(
                    q, keys[b, :, pair_cols], (((1,), (1,)), ((), ())), preferred_element_type=F32
                )
                scores = jnp.where(places < misc[2, b : b + 1, 0:1], scores, MASKED)
                top = jnp.max(scores, axis=1, keepdims=True)
                weight = jnp.exp2((scores - top) * exponent)
                total = jnp.sum(weight, axis=1, keepdims=True)
                summed = jnp.dot(
                    weight.astype(BF16), values[b, :, pair_cols], preferred_element_type=F32
                )
                sums.append(summed.reshape(GROUP, tokens, 2 * HEAD_DIM))
                wide_shape = (GROUP * tokens, LANES)
                tops.append(
                    jnp.broadcast_to(top * scale, wide_shape).reshape(GROUP, tokens, LANES)
                )
                totals.append(jnp.broadcast_to(total, wide_shape).reshape(GROUP, tokens, LANES))
            for p in range(2):
                k = 2 * c + p
                owner = first_owner + k
                low, high = (0, 1) if p == 0 else (1, 0)
                own = slice(p * HEAD_DIM, (p + 1) * HEAD_DIM)
                summed = jnp.where(upper, sums[low][:, :, own], sums[high][:, :, own])
                top = jnp.where(upper, tops[low], tops[high])
                total = jnp.where(upper, totals[low], totals[high])
                stats = jnp.zeros((tokens, LANES), F32)
                for i, piece in enumerate(pieces_of(top, 3) + pieces_of(total, 3)):
                    for g in range(GROUP):
                        stats = jnp.where(lane == g * 8 + i, piece[g], stats)
                part_out[k, :GROUP] = summed.astype(BF16)
                part_out[k, GROUP] = stats.astype(BF16)
        for c in order[2 * near : 2 * near + 2]:
            for p in range(2):
                k = 2 * c + p
                owner = first_owner + k

                @pl.when(owner != me)
                def _():
                    copy_to(3, part_out.at[k], part_in, me, owner).start()

    @pl.when(is_owner)
    def _():
        part_in[me] = part_out[mine]
        departed(2, joint_in.at[others, pl.ds(0, GROUP)])
        landed(3, part_in.at[others])
        stats = part_in[:, GROUP].astype(F32).reshape(n * tokens, LANES).astype(BF16)
        stats = jnp.dot(stats, spread[...], preferred_element_type=F32)
        swap = jnp.full((tokens, LANES), mine % 2, jnp.int32) == 1
        for g in range(GROUP):
            tops = stats[:, g * LANES : (g + 1) * LANES].reshape(n, tokens, LANES)
            totals = stats[:, (GROUP + g) * LANES : (GROUP + g + 1) * LANES]
            totals = totals.reshape(n, tokens, LANES)
            top = fresh[1, g]
            for j in range(n):
                top = jnp.maximum(top, tops[j])
            factor = jnp.exp(fresh[1, g] - top)
            total = fresh[2, g] * factor
            summed = fresh[0, g] * factor
            for j in range(n):
                factor = jnp.exp(tops[j] - top)
                total += totals[j] * factor
                summed += part_in[j, g].astype(F32) * factor
            x = summed / total
            x = jnp.where(swap, pltpu.roll(x, steps, 0), x)
            attended_all[mine, g] = x.astype(BF16)
        each_peer(lambda peer: copy_to(4, attended_all.at[mine], attended_all, mine, peer, mine).start())

    departed_to_owners(3, part_out)

    loads[4].wait()
    projected = jnp.zeros((tokens, cols), F32)
    for c in order:
        for p in range(2):
            k = 2 * c + p

            @pl.when(first_owner + k != me)
            def _():
                landed(4, attended_all.at[k], k)

        x = jnp.concatenate(
            [attended_all[2 * c + p, g] for p in range(2) for g in range(GROUP)], axis=1
        )
        at = pl.ds(pl.multiple_of(c * 2 * group_width, LANES), 2 * group_width)
        wide[:, at] = x.astype(F32)
        projected += lax.dot_general(
            x, w_out[:, at], (((1,), (1,)), ((), ())), preferred_element_type=F32
        )
    mid = stream + projected
    square = jnp.sum(mid * mid, axis=1, keepdims=True)
    spare = block_width - cols
    at = lax.broadcasted_iota(jnp.int32, (tokens, spare), 1)
    extra = jnp.zeros((tokens, spare), F32)
    for i, piece in enumerate(pieces_of(square, 3)):
        extra = jnp.where(at == i, piece, extra)
    mid_all[me, :, :cols] = (mid * gain[1:2]).astype(BF16)
    mid_all[me, :, cols:] = extra.astype(BF16)
    if staged:
        for d in range(n - 1, 0, -1):
            copy_to(5, mid_all.at[me], mid_all, me, partner(d), arrival_of(d)).start()
    else:
        each_peer(lambda peer: copy_to(5, mid_all.at[me], mid_all, me, peer).start())

    for s in range(steps):
        attended_ref[s] = interleaved(s, width)

    @pl.when(is_owner)
    def _():
        departed(4, joint_in.at[others, pl.ds(0, GROUP)])

    loads[5].wait()
    loads[6].wait()
    quad = 4
    gate = jnp.zeros((tokens, units), F32)
    upper_units = jnp.zeros((tokens, units), F32)
    tail = jnp.zeros((tokens, spare), F32)
    if staged:
        batches_of = [(0,), (1,), (2, 3)] + [
            tuple(range(q * quad, (q + 1) * quad)) for q in range(1, n // quad)
        ]
        for members in batches_of:
            if members[0]:
                start = partner(members[0]) // len(members) * len(members)
                landed(5, mid_all.at[pl.ds(start, len(members))], arrival_of(members[0]))
            for d in members:
                j = partner(d)
                x = mid_all[j]
                tail += x[:, cols:].astype(F32)
                x = x[:, :cols]
                at = pl.ds(pl.multiple_of(j * cols, 16), cols)
                gate += jnp.dot(x, w_gate[at, :], preferred_element_type=F32)
                upper_units += jnp.dot(x, w_up[at, :], preferred_element_type=F32)
    else:
        landed(5, mid_all.at[others])
        for j in range(n):
            x = mid_all[j].astype(F32)
            tail += x[:, cols:]
            wide[:, j * cols : (j + 1) * cols] = x[:, :cols]
        x = wide[...].astype(BF16)
        gate = jnp.dot(x, w_gate[...], preferred_element_type=F32)
        upper_units = jnp.dot(x, w_up[...], preferred_element_type=F32)
    square = jnp.sum(tail[:, :3], axis=1, keepdims=True)
    factor = lax.rsqrt(square / width + NORM_EPS)
    gate = gate * factor
    upper_units = upper_units * factor
    hidden = (gate / (1.0 + jnp.exp(-gate)) * upper_units).astype(BF16)
    loads[7].wait()

    if staged:
        for q in range(n // quad - 1, -1, -1):
            base = partner(q * quad) // quad * quad
            at = pl.ds(pl.multiple_of(base * cols, LANES), quad * cols)
            part = jnp.dot(hidden, w_down[:, at], preferred_element_type=F32)
            for i in range(quad):
                j = base + i
                down_out[j] = part[:, i * cols : (i + 1) * cols].astype(BF16)
                if q:
                    copy_to(6, down_out.at[j], down_in, me, j).start()
                else:

                    @pl.when(j != me)
                    def _():
                        copy_to(6, down_out.at[j], down_in, me, j).start()

    else:
        wide[...] = jnp.dot(hidden, w_down[...], preferred_element_type=F32)
        for j in range(n):
            down_out[j] = wide[:, j * cols : (j + 1) * cols].astype(BF16)
        each_peer(lambda peer: copy_to(6, down_out.at[peer], down_in, me, peer).start())
    down_in[me] = down_out[me]
    departed(5, mid_all.at[others])
    landed(6, down_in.at[others])
    summed = down_in[0].astype(F32)
    for j in range(1, n):
        summed += down_in[j].astype(F32)
    wide[:, :cols] = mid + summed
    for s in range(steps):
        layer_ref[s] = interleaved(s, cols)
    departed(6, down_in.at[others])


def finish_kernel(attended, layer, attended_out, layer_out, sem):
    copies = [
        pltpu.make_async_copy(attended, attended_out, sem.at[0]),
        pltpu.make_async_copy(layer, layer_out, sem.at[1]),
    ]
    for copy in copies:
        copy.start()
    for copy in copies:
        copy.wait()


def body(
    token_ids,
    lengths,
    embed_table,
    attn_gain,
    w_qkv,
    qkv_bias,
    cache_keys,
    cache_values,
    w_out,
    mlp_gain,
    w_gate,
    w_up,
    w_down,
):
    n = lax.axis_size("seq")
    steps, batches = token_ids.shape
    tokens = steps * batches
    width = embed_table.shape[1]
    cols = w_out.shape[1]
    block_width = -(-(cols + 3) // LANES) * LANES
    vmem = pl.BlockSpec(memory_space=pltpu.VMEM)
    hbm = pl.BlockSpec(memory_space=pltpu.HBM)

    def in_hbm(a):
        return pltpu.with_memory_space_constraint(a, pltpu.HBM)

    def in_vmem(a):
        return pltpu.with_memory_space_constraint(a, pltpu.VMEM)

    blocks, gains, misc = pl.pallas_call(
        functools.partial(gather_kernel, n),
        out_shape=(
            pltpu.VMEM((n, tokens, block_width), BF16),
            pltpu.VMEM((n, 8, cols), F32),
            pltpu.VMEM((3, tokens, LANES), F32),
        ),
        in_specs=[hbm] * 5,
        out_specs=(vmem, vmem, vmem),
        scratch_shapes=[
            pltpu.SMEM((batches, steps), jnp.int32),
            pltpu.SMEM((batches,), jnp.int32),
            pltpu.VMEM((width,), BF16),
            pltpu.VMEM((width,), BF16),
            pltpu.VMEM((tokens, 8, width), BF16),
            pltpu.VMEM((tokens, width), F32),
            pltpu.SemaphoreType.DMA((4,)),
            pltpu.SemaphoreType.DMA((tokens,)),
        ],
        compiler_params=pltpu.CompilerParams(vmem_limit_bytes=60 * 1024 * 1024),
    )(*(in_hbm(a) for a in (token_ids.T, lengths, attn_gain, mlp_gain, embed_table)))
    joint_heads = HEADS + 2 * KV_HEADS
    attended, layer_out = pl.pallas_call(
        functools.partial(layer_kernel, n),
        out_shape=(
            pltpu.VMEM((steps, batches, width), BF16),
            pltpu.VMEM((steps, batches, cols), BF16),
        ),
        in_specs=[vmem] * 3 + [hbm] * 8,
        out_specs=(vmem, vmem),
        scratch_shapes=[
            pltpu.VMEM((joint_heads, HEAD_DIM), F32),
        ]
        + [
            pltpu.VMEM(a.shape, a.dtype)
            for a in (w_qkv, cache_keys, cache_values, w_out.T, w_gate, w_up, w_down)
        ]
        + [
            pltpu.VMEM((n, tokens, block_width), BF16),
            pltpu.VMEM((KV_HEADS, LOCAL, tokens, LANES), BF16),
            pltpu.VMEM((n, LOCAL, tokens, LANES), BF16),
            pltpu.VMEM((KV_HEADS, GROUP, tokens, LANES), BF16),
            pltpu.VMEM((LOCAL, tokens, LANES), F32),
            pltpu.VMEM((KV_HEADS, GROUP + 1, tokens, LANES), BF16),
            pltpu.VMEM((n, GROUP + 1, tokens, LANES), BF16),
            pltpu.VMEM((3, GROUP, tokens, LANES), F32),
            pltpu.VMEM((LANES, 2 * GROUP * LANES), BF16),
            pltpu.VMEM((KV_HEADS, GROUP, tokens, LANES), BF16),
            pltpu.VMEM((n, tokens, block_width), BF16),
            pltpu.VMEM((tokens, width), F32),
            pltpu.VMEM((n, tokens, cols), BF16),
            pltpu.VMEM((n, tokens, cols), BF16),
            pltpu.SemaphoreType.DMA((8,)),
            pltpu.SemaphoreType.DMA((7,)),
            pltpu.SemaphoreType.DMA((RECEIVES,)),
        ],
        compiler_params=pltpu.CompilerParams(
            collective_id=0, has_side_effects=True, vmem_limit_bytes=57 * 1024 * 1024
        ),
    )(
        *(in_vmem(a) for a in (blocks, gains, misc)),
        *(
            in_hbm(a)
            for a in (
                qkv_bias.reshape(joint_heads, HEAD_DIM),
                w_qkv,
                cache_keys,
                cache_values,
                w_out.T,
                w_gate,
                w_up,
                w_down,
            )
        ),
    )
    return pl.pallas_call(
        finish_kernel,
        out_shape=(
            jax.ShapeDtypeStruct(attended.shape, BF16),
            jax.ShapeDtypeStruct(layer_out.shape, BF16),
        ),
        in_specs=[vmem, vmem],
        out_specs=(hbm, hbm),
        scratch_shapes=[pltpu.SemaphoreType.DMA((2,))],
        compiler_params=pltpu.CompilerParams(vmem_limit_bytes=60 * 1024 * 1024),
    )(in_vmem(attended), in_vmem(layer_out))


def solution(mesh):
    return jax.shard_map(
        body,
        mesh=mesh,
        in_specs=(
            P(None, "parts"),
            P("parts"),
            P("seq", None),
            P(),
            P("seq", None),
            P(),
            P("parts", "seq", None),
            P("parts", "seq", None),
            P(None, "seq"),
            P(),
            P(None, "seq"),
            P(None, "seq"),
            P("seq", None),
        ),
        out_specs=(P(None, "parts", None), P(None, "parts", "seq")),
        check_vma=False,
    )
```

time: 78.7 us -> 49.1 us (0.62)
  Pallas kernels: 68.4 us -> 48.2 us
  local copies, waits for them, and re-layouts: 6.37 us -> 0 us
  other arithmetic: 2.84 us -> 0 us
    pallas_call x1 -> x3, Pallas kernels: 68.4 us -> 48.2 us  [the longest x1 45.1 us: body(): pl.pallas_call(functools.partial(layer_kernel, n), out_shape=(pltpu.VMEM(...]
    reshape x2 -> x0, local copies, waits for them, and re-layouts: 2.85 us -> none  [the longest x1 1.56 us: body(): attended.reshape(step_count, batch_count, width)]
    gather x1 -> x0, local copies, waits for them, and re-layouts: 2.49 us -> none  [body(): embed_table.at[jnp.clip(local_ids, 0, vocab_rows - 1)]]
    convert_element_type x2 -> x0, other arithmetic: 1.35 us -> none  [the longest x1 0.69 us: body(): inside.astype(F32)[:, None]]
    convert_element_type x3 -> x0, local copies, waits for them, and re-layouts: 0.85 us -> none  [the longest x2 0.76 us: body(): inside.astype(F32)[:, None]]
where the time goes in v1:
time: 49.1 us; the launch traced here: 48.8 us
  Pallas kernels  48.2 us (98%)
  between operations  0.65 us (1%)
    pallas_call x1, Pallas kernels, body(): pl.pallas_call(functools.partial(layer_kernel, n), out_shape=(pltpu.VMEM(...  45.1 us
    pallas_call x1, Pallas kernels, body(): pl.pallas_call(functools.partial(gather_kernel, n), out_shape=(pltpu.VMEM...  2.4 us

profile of v1, /device:TPU:0, one launch (start us, length us, event | category | flops | bytes accessed | tf_op | source)
XLA Modules:
  0.0 48.8 jit_solution(9212232021942635397)
XLA Ops:
  0.6 2.4 %shard_map.140 = (bf16[16,8,384]{2,1,0:T(8,128)(2,1)S(1)}, f32[16,8,320]{2,1,0:T(8,128)S(1)}, f32[3,8,128]{2,1,0:T(8,128)S(1)}) custom-call(s32[2,4]{1,0:T(2,128)} %bitcast.5, s32[2]{0:T(128)} %lengths_hbm.1, bf16[5120]{0:T(1024)(128)(2,1)} %gain_one_hbm.1, bf16[5120]{0:T(1024)(128)(2,1)} %gain_two_hbm.1, bf16[4752,5120]{1,0:T(8,128)(2,1)} %table.1), custom_call_target="tpu_custom_call" | custom-call | tf_op jit(solution)/shard_map/pallas_call | solution.py:636
  3.0 45.1 %shard_map.141 = (bf16[4,2,5120]{2,1,0:T(2,128)(2,1)S(1)}, bf16[4,2,320]{2,1,0:T(2,128)(2,1)S(1)}) custom-call(bf16[16,8,384]{2,1,0:T(8,128)(2,1)S(1)} %get-tuple-element.7.blocks, f32[16,8,320]{2,1,0:T(8,128)S(1)} %get-tuple-element.8.gains, f32[3,8,128]{2,1,0:T(8,128)S(1)} %get-tuple-element.9.misc, f32[56,128]{1,0:T(8,128)} %bitcast.4, ...), custom_call_target="tpu_custom_call" | custom-call | tf_op jit(solution)/shard_map/pallas_call | solution.py:658
  48.2 0.7 %shard_map.142 = (bf16[4,2,5120]{2,1,0:T(2,128)(2,1)}, bf16[4,2,320]{2,1,0:T(2,128)(2,1)}) custom-call(bf16[4,2,5120]{2,1,0:T(2,128)(2,1)S(1)} %get-tuple-element.10.attended, bf16[4,2,320]{2,1,0:T(2,128)(2,1)S(1)} %get-tuple-element.11.layer), custom_call_target="tpu_custom_call" | custom-call | tf_op jit(solution)/shard_map/pallas_call | solution.py:711

commit v2 on v1

--- a/solution.py
+++ b/solution.py
@@ -23,8 +23,9 @@
 BF16 = jnp.bfloat16
 MESH = pl.DeviceIdType.MESH
 
-FIRST_RECEIVE = (0, 1, 2, 2 + KV_HEADS, 3 + KV_HEADS, 3 + 2 * KV_HEADS, 11 + 2 * KV_HEADS)
-RECEIVES = 12 + 2 * KV_HEADS
+PAIRS = KV_HEADS // 2
+FIRST_RECEIVE = (0, 1, 2, 2 + PAIRS, 3 + PAIRS, 3 + 2 * PAIRS, 8 + 2 * PAIRS)
+RECEIVES = 9 + 2 * PAIRS
 
 
 def pieces_of(value, count):
@@ -167,6 +168,7 @@
     wide,
     down_out,
     down_in,
+    held,
     load_sem,
     send_sem,
     recv_sem,
@@ -178,12 +180,15 @@
     steps = tokens // batches
     cols, width = w_out.shape
     units = w_gate.shape[1]
-    pairs = KV_HEADS // 2
     group_width = GROUP * HEAD_DIM
     scale = 1.0 / math.sqrt(HEAD_DIM)
-    first_owner = n // 2 - KV_HEADS // 2
-    is_owner = (me >= first_owner) & (me < first_owner + KV_HEADS)
-    mine = jnp.clip(me - first_owner, 0, KV_HEADS - 1)
+    first_owner = n // 2 - PAIRS
+    is_owner = (me >= first_owner) & (me < first_owner + 2 * PAIRS) & (me % 2 == 1)
+    mine = jnp.clip((me - first_owner) // 2, 0, PAIRS - 1)
+
+    def owner_of(c):
+        return first_owner + 2 * c + 1
+
     side = me // (n // 2)
     turn = (me // 2) % 2
 
@@ -214,7 +219,7 @@
         load.start()
 
     unrolled = n & (n - 1) == 0 and n <= 32
-    staged = unrolled and n // 4 <= 6 and cols % 16 == 0 and (4 * cols) % LANES == 0
+    staged = unrolled and n // 4 <= 4 and cols % 16 == 0 and (4 * cols) % LANES == 0
     bits = n.bit_length() - 1
     flips = [(1 << k) * (1 - 2 * ((me // (1 << k)) % 2)) for k in range(bits)]
 
@@ -238,7 +243,7 @@
         return pltpu.make_async_remote_copy(
             src_ref=source,
             dst_ref=target.at[slot],
-            send_sem=send_sem.at[step],
+            send_sem=send_sem.at[step % 2],
             recv_sem=recv_sem.at[FIRST_RECEIVE[step] + arrival],
             device_id={"seq": peer},
             device_id_type=MESH,
@@ -248,7 +253,7 @@
         return pltpu.make_async_remote_copy(
             src_ref=whole,
             dst_ref=whole,
-            send_sem=send_sem.at[step],
+            send_sem=send_sem.at[step % 2],
             recv_sem=recv_sem.at[FIRST_RECEIVE[step] + arrival],
             device_id={"seq": lax.rem(me + 1, n)},
             device_id_type=MESH,
@@ -263,11 +268,11 @@
     def departed_to_owners(step, target):
         @pl.when(is_owner)
         def _():
-            departed(step, target.at[pl.ds(0, KV_HEADS - 1)])
+            departed(step, target.at[pl.ds(0, PAIRS - 1)])
 
         @pl.when(jnp.logical_not(is_owner))
         def _():
-            departed(step, target.at[pl.ds(0, KV_HEADS)])
+            departed(step, target.at[pl.ds(0, PAIRS)])
 
     others = pl.ds(0, n - 1)
 
@@ -301,35 +306,35 @@
 
     loads[0].wait()
     loads[1].wait()
-    for i in range(pairs):
-        c = side * i + (1 - side) * (pairs - 1 - i)
-        q_part = jnp.dot(
+    def joint_part(at, count):
+        return jnp.dot(
             normed,
-            w_qkv[:, pl.ds(pl.multiple_of(c * 2 * group_width, LANES), 2 * group_width)],
+            w_qkv[:, pl.ds(pl.multiple_of(at * LANES, LANES), count * LANES)],
             preferred_element_type=F32,
-        )
-        k_part = jnp.dot(
-            normed,
-            w_qkv[:, pl.ds(pl.multiple_of((HEADS + 2 * c) * LANES, LANES), 2 * LANES)],
-            preferred_element_type=F32,
-        )
-        v_part = jnp.dot(
-            normed,
-            w_qkv[:, pl.ds(pl.multiple_of((HEADS + KV_HEADS + 2 * c) * LANES, LANES), 2 * LANES)],
-            preferred_element_type=F32,
-        )
-        for p in range(2):
-            k = 2 * c + p
-            owner = first_owner + k
-            for g in range(GROUP):
-                at = p * group_width + g * LANES
-                joint_out[k, g] = q_part[:, at : at + LANES].astype(BF16)
-            joint_out[k, GROUP] = k_part[:, p * LANES : (p + 1) * LANES].astype(BF16)
-            joint_out[k, GROUP + 1] = v_part[:, p * LANES : (p + 1) * LANES].astype(BF16)
-
-            @pl.when(owner != me)
+        ).astype(BF16)
+
+    far_first = [side * i + (1 - side) * (PAIRS - 1 - i) for i in range(PAIRS)]
+    parts = None
+    for i in range(PAIRS + 1):
+        ready = parts
+        if i < PAIRS:
+            c = far_first[i]
+            parts = (
+                joint_part(2 * GROUP * c, 2 * GROUP),
+                joint_part(HEADS + 2 * c, 2),
+                joint_part(HEADS + KV_HEADS + 2 * c, 2),
+            )
+        if i:
+            c = far_first[i - 1]
+            for part, count, to in zip(ready, (GROUP, 1, 1), (0, GROUP, GROUP + 1)):
+                for p in range(2):
+                    for g in range(count):
+                        at = (p * count + g) * LANES
+                        joint_out[c, p, to + g] = part[:, at : at + LANES]
+
+            @pl.when(owner_of(c) != me)
             def _():
-                copy_to(1, joint_out.at[k], joint_in, me, owner).start()
+                copy_to(1, joint_out.at[c], joint_in, me, owner_of(c)).start()
 
     departed(0, rows_in.at[others])
 
@@ -337,47 +342,49 @@
     def _():
         joint_in[me] = joint_out[mine]
         landed(1, joint_in.at[others])
-        joint = joint_in[0].astype(F32)
-        for j in range(1, n):
-            joint += joint_in[j].astype(F32)
-        odd = mine % 2
-        swap = jnp.full((tokens, LANES), odd, jnp.int32) == 1
         cos, sin = misc[0], misc[1]
 
-        def biased(i, h):
-            return (joint[i] + bias[pl.ds(h, 1), :]).astype(BF16).astype(F32)
+        def biased(p, i, h):
+            joint = joint_in[0, p, i].astype(F32)
+            for j in range(1, n):
+                joint += joint_in[j, p, i].astype(F32)
+            return (joint + bias[pl.ds(h, 1), :]).astype(BF16).astype(F32)
 
         def turned(x):
             x = x * cos + pltpu.roll(x, HEAD_DIM // 2, 1) * sin
             return x.astype(BF16).astype(F32)
 
-        for g in range(GROUP):
-            x = turned(biased(g, mine * GROUP + g))
-            x = jnp.where(swap, pltpu.roll(x, steps, 0), x)
-            own_heads[g] = x
-            heads_all[mine, g] = x.astype(BF16)
+        for p in range(2):
+            k = 2 * mine + p
+            for g in range(GROUP):
+                x = turned(biased(p, g, k * GROUP + g))
+                x = pltpu.roll(x, steps, 0) if p else x
+                own_heads[p, g] = x
+                heads_all[mine, p, g] = x.astype(BF16)
         each_peer(lambda peer: copy_to(2, heads_all.at[mine], heads_all, mine, peer, mine).start())
-        own_heads[GROUP] = turned(biased(GROUP, HEADS + mine))
-        own_heads[GROUP + 1] = biased(GROUP + 1, HEADS + KV_HEADS + mine)
-
-        q = own_heads[:GROUP].reshape(GROUP * tokens, HEAD_DIM).astype(BF16)
-        new_keys = own_heads[GROUP].astype(BF16)
-        new_values = own_heads[GROUP + 1].astype(BF16)
-        shape = (GROUP * tokens, tokens)
-        at = lax.broadcasted_iota(jnp.int32, shape, 0) % tokens
-        other = lax.broadcasted_iota(jnp.int32, shape, 1)
-        prompt = (at // steps + odd) % 2
-        seen = (other // steps == prompt) & (other % steps <= at % steps)
-        score = lax.dot_general(q, new_keys, (((1,), (1,)), ((), ())), preferred_element_type=F32)
-        score = jnp.where(seen, score * scale, MASKED)
-        top = jnp.max(score, axis=1, keepdims=True)
-        weight = jnp.where(seen, jnp.exp(score - top), 0.0)
-        total = jnp.sum(weight, axis=1, keepdims=True)
-        summed = jnp.dot(weight.astype(BF16), new_values, preferred_element_type=F32)
-        wide_shape = (GROUP, tokens, LANES)
-        fresh[0] = summed.reshape(wide_shape)
-        fresh[1] = jnp.broadcast_to(top, (GROUP * tokens, LANES)).reshape(wide_shape)
-        fresh[2] = jnp.broadcast_to(total, (GROUP * tokens, LANES)).reshape(wide_shape)
+
+        for p in range(2):
+            k = 2 * mine + p
+            new_keys = turned(biased(p, GROUP, HEADS + k)).astype(BF16)
+            new_values = biased(p, GROUP + 1, HEADS + KV_HEADS + k).astype(BF16)
+            q = own_heads[p].reshape(GROUP * tokens, HEAD_DIM).astype(BF16)
+            shape = (GROUP * tokens, tokens)
+            at = lax.broadcasted_iota(jnp.int32, shape, 0) % tokens
+            other = lax.broadcasted_iota(jnp.int32, shape, 1)
+            prompt = (at // steps + p) % 2
+            seen = (other // steps == prompt) & (other % steps <= at % steps)
+            score = lax.dot_general(
+                q, new_keys, (((1,), (1,)), ((), ())), preferred_element_type=F32
+            )
+            score = jnp.where(seen, score * scale, MASKED)
+            top = jnp.max(score, axis=1, keepdims=True)
+            weight = jnp.where(seen, jnp.exp(score - top), 0.0)
+            total = jnp.sum(weight, axis=1, keepdims=True)
+            summed = jnp.dot(weight.astype(BF16), new_values, preferred_element_type=F32)
+            fresh[0, p] = summed.reshape(GROUP, tokens, LANES)
+            for i, x in ((1, top), (2, total)):
+                x = jnp.broadcast_to(x, (GROUP * tokens, LANES))
+                fresh[i, p] = x.reshape(GROUP, tokens, LANES)
 
     departed_to_owners(1, joint_out)
 
@@ -387,112 +394,118 @@
         me * local_len + lax.broadcasted_iota(jnp.int32, (1, local_len), 1)
     ).astype(F32)
     exponent = scale / math.log(2.0)
-    order = [
-        2 * side + turn,
-        2 * side + 1 - turn,
-        2 * (1 - side) + turn,
-        2 * (1 - side) + 1 - turn,
-    ]
-    for near in range(2):
-        for c in order[2 * near : 2 * near + 2]:
-            for p in range(2):
-                k = 2 * c + p
-
-                @pl.when(first_owner + k != me)
+    near = [2 * side + turn, 2 * side + 1 - turn]
+    far = [2 * (1 - side) + turn, 2 * (1 - side) + 1 - turn]
+    order = [near[0], far[0], far[1], near[1]]
+    def pair_cols(c):
+        return pl.ds(pl.multiple_of(c * 2 * HEAD_DIM, LANES), 2 * HEAD_DIM)
+
+    def scored(c, slot, b):
+        chosen = upper if b == 0 else ~upper
+        first = heads_all[c, 0].astype(F32)
+        second = heads_all[c, 1].astype(F32)
+        q = jnp.concatenate(
+            [jnp.where(chosen, first, 0.0), jnp.where(chosen, 0.0, second)], axis=2
+        )
+        q = q.reshape(GROUP * tokens, 2 * HEAD_DIM).astype(BF16)
+        scores = lax.dot_general(
+            q, keys[b, :, pair_cols(c)], (((1,), (1,)), ((), ())), preferred_element_type=F32
+        )
+        scores = jnp.where(places < misc[2, b : b + 1, 0:1], scores, MASKED)
+        held[slot, b] = scores
+        return jnp.max(scores, axis=1, keepdims=True)
+
+    def softened(slot, b, top):
+        weight = jnp.exp2((held[slot, b] - top) * exponent)
+        return weight.astype(BF16), jnp.sum(weight, axis=1, keepdims=True)
+
+    def product(c, b, weight):
+        summed = jnp.dot(weight, values[b, :, pair_cols(c)], preferred_element_type=F32)
+        return summed.reshape(GROUP, tokens, 2 * HEAD_DIM)
+
+    def packed(c, sums, tops, totals):
+        def widened(x):
+            return jnp.broadcast_to(x, (GROUP * tokens, LANES)).reshape(GROUP, tokens, LANES)
+
+        tops = [widened(top * scale) for top in tops]
+        totals = [widened(total) for total in totals]
+        for p in range(2):
+            low, high = (0, 1) if p == 0 else (1, 0)
+            own = slice(p * HEAD_DIM, (p + 1) * HEAD_DIM)
+            summed = jnp.where(upper, sums[low][:, :, own], sums[high][:, :, own])
+            top = jnp.where(upper, tops[low], tops[high])
+            total = jnp.where(upper, totals[low], totals[high])
+            stats = jnp.zeros((tokens, LANES), F32)
+            for i, piece in enumerate(pieces_of(top, 3) + pieces_of(total, 3)):
+                for g in range(GROUP):
+                    stats = jnp.where(lane == g * 8 + i, piece[g], stats)
+            part_out[c, p, :GROUP] = summed.astype(BF16)
+            part_out[c, p, GROUP] = stats.astype(BF16)
+
+    found = {}
+    for block in ((0,), (1, 2), (3, 4)):
+        for r in block:
+            if r < PAIRS:
+
+                @pl.when(owner_of(order[r]) != me)
                 def _():
-                    landed(2, heads_all.at[k], k)
-
-        for c in order[2 * near : 2 * near + 2]:
-            first = heads_all[2 * c].astype(F32)
-            second = heads_all[2 * c + 1].astype(F32)
-            pair_cols = pl.ds(pl.multiple_of(c * 2 * HEAD_DIM, LANES), 2 * HEAD_DIM)
-            sums, tops, totals = [], [], []
-            for b in range(batches):
-                chosen = upper if b == 0 else ~upper
-                q = jnp.concatenate(
-                    [jnp.where(chosen, first, 0.0), jnp.where(chosen, 0.0, second)], axis=2
-                )
-                q = q.reshape(GROUP * tokens, 2 * HEAD_DIM).astype(BF16)
-                scores = lax.dot_general(
-                    q, keys[b, :, pair_cols], (((1,), (1,)), ((), ())), preferred_element_type=F32
-                )
-                scores = jnp.where(places < misc[2, b : b + 1, 0:1], scores, MASKED)
-                top = jnp.max(scores, axis=1, keepdims=True)
-                weight = jnp.exp2((scores - top) * exponent)
-                total = jnp.sum(weight, axis=1, keepdims=True)
-                summed = jnp.dot(
-                    weight.astype(BF16), values[b, :, pair_cols], preferred_element_type=F32
-                )
-                sums.append(summed.reshape(GROUP, tokens, 2 * HEAD_DIM))
-                wide_shape = (GROUP * tokens, LANES)
-                tops.append(
-                    jnp.broadcast_to(top * scale, wide_shape).reshape(GROUP, tokens, LANES)
-                )
-                totals.append(jnp.broadcast_to(total, wide_shape).reshape(GROUP, tokens, LANES))
-            for p in range(2):
-                k = 2 * c + p
-                owner = first_owner + k
-                low, high = (0, 1) if p == 0 else (1, 0)
-                own = slice(p * HEAD_DIM, (p + 1) * HEAD_DIM)
-                summed = jnp.where(upper, sums[low][:, :, own], sums[high][:, :, own])
-                top = jnp.where(upper, tops[low], tops[high])
-                total = jnp.where(upper, totals[low], totals[high])
-                stats = jnp.zeros((tokens, LANES), F32)
-                for i, piece in enumerate(pieces_of(top, 3) + pieces_of(total, 3)):
-                    for g in range(GROUP):
-                        stats = jnp.where(lane == g * 8 + i, piece[g], stats)
-                part_out[k, :GROUP] = summed.astype(BF16)
-                part_out[k, GROUP] = stats.astype(BF16)
-        for c in order[2 * near : 2 * near + 2]:
-            for p in range(2):
-                k = 2 * c + p
-                owner = first_owner + k
-
-                @pl.when(owner != me)
+                    landed(2, heads_all.at[order[r]], order[r])
+
+        for r in block:
+            before = r - 1
+            if r < PAIRS:
+                found[r] = [scored(order[r], r % 2, b) for b in range(batches)]
+            if r:
+                soft = [softened(before % 2, b, found[before][b]) for b in range(batches)]
+                sums = [product(order[before], b, soft[b][0]) for b in range(batches)]
+                packed(order[before], sums, found[before], [x[1] for x in soft])
+        for r in block:
+            if r:
+                c = order[r - 1]
+
+                @pl.when(owner_of(c) != me)
                 def _():
-                    copy_to(3, part_out.at[k], part_in, me, owner).start()
+                    copy_to(3, part_out.at[c], part_in, me, owner_of(c)).start()
 
     @pl.when(is_owner)
     def _():
         part_in[me] = part_out[mine]
-        departed(2, joint_in.at[others, pl.ds(0, GROUP)])
+        departed(2, joint_in.at[others, :, pl.ds(0, GROUP)])
         landed(3, part_in.at[others])
-        stats = part_in[:, GROUP].astype(F32).reshape(n * tokens, LANES).astype(BF16)
-        stats = jnp.dot(stats, spread[...], preferred_element_type=F32)
-        swap = jnp.full((tokens, LANES), mine % 2, jnp.int32) == 1
-        for g in range(GROUP):
-            tops = stats[:, g * LANES : (g + 1) * LANES].reshape(n, tokens, LANES)
-            totals = stats[:, (GROUP + g) * LANES : (GROUP + g + 1) * LANES]
-            totals = totals.reshape(n, tokens, LANES)
-            top = fresh[1, g]
-            for j in range(n):
-                top = jnp.maximum(top, tops[j])
-            factor = jnp.exp(fresh[1, g] - top)
-            total = fresh[2, g] * factor
-            summed = fresh[0, g] * factor
-            for j in range(n):
-                factor = jnp.exp(tops[j] - top)
-                total += totals[j] * factor
-                summed += part_in[j, g].astype(F32) * factor
-            x = summed / total
-            x = jnp.where(swap, pltpu.roll(x, steps, 0), x)
-            attended_all[mine, g] = x.astype(BF16)
+        for p in range(2):
+            stats = part_in[:, p, GROUP].astype(F32).reshape(n * tokens, LANES).astype(BF16)
+            stats = jnp.dot(stats, spread[...], preferred_element_type=F32)
+            for g in range(GROUP):
+                tops = stats[:, g * LANES : (g + 1) * LANES].reshape(n, tokens, LANES)
+                totals = stats[:, (GROUP + g) * LANES : (GROUP + g + 1) * LANES]
+                totals = totals.reshape(n, tokens, LANES)
+                top = fresh[1, p, g]
+                for j in range(n):
+                    top = jnp.maximum(top, tops[j])
+                factor = jnp.exp(fresh[1, p, g] - top)
+                total = fresh[2, p, g] * factor
+                summed = fresh[0, p, g] * factor
+                for j in range(n):
+                    factor = jnp.exp(tops[j] - top)
+                    total += totals[j] * factor
+                    summed += part_in[j, p, g].astype(F32) * factor
+                x = summed / total
+                x = pltpu.roll(x, steps, 0) if p else x
+                attended_all[mine, p, g] = x.astype(BF16)
         each_peer(lambda peer: copy_to(4, attended_all.at[mine], attended_all, mine, peer, mine).start())
 
     departed_to_owners(3, part_out)
 
     loads[4].wait()
     projected = jnp.zeros((tokens, cols), F32)
-    for c in order:
-        for p in range(2):
-            k = 2 * c + p
-
-            @pl.when(first_owner + k != me)
-            def _():
-                landed(4, attended_all.at[k], k)
+    for c in near + far:
+
+        @pl.when(owner_of(c) != me)
+        def _():
+            landed(4, attended_all.at[c], c)
 
         x = jnp.concatenate(
-            [attended_all[2 * c + p, g] for p in range(2) for g in range(GROUP)], axis=1
+            [attended_all[c, p, g] for p in range(2) for g in range(GROUP)], axis=1
         )
         at = pl.ds(pl.multiple_of(c * 2 * group_width, LANES), 2 * group_width)
         wide[:, at] = x.astype(F32)
@@ -519,7 +532,7 @@
 
     @pl.when(is_owner)
     def _():
-        departed(4, joint_in.at[others, pl.ds(0, GROUP)])
+        departed(4, joint_in.at[others, :, pl.ds(0, GROUP)])
 
     loads[5].wait()
     loads[6].wait()
@@ -672,25 +685,26 @@
         ]
         + [
             pltpu.VMEM((n, tokens, block_width), BF16),
-            pltpu.VMEM((KV_HEADS, LOCAL, tokens, LANES), BF16),
-            pltpu.VMEM((n, LOCAL, tokens, LANES), BF16),
-            pltpu.VMEM((KV_HEADS, GROUP, tokens, LANES), BF16),
-            pltpu.VMEM((LOCAL, tokens, LANES), F32),
-            pltpu.VMEM((KV_HEADS, GROUP + 1, tokens, LANES), BF16),
-            pltpu.VMEM((n, GROUP + 1, tokens, LANES), BF16),
-            pltpu.VMEM((3, GROUP, tokens, LANES), F32),
+            pltpu.VMEM((PAIRS, 2, LOCAL, tokens, LANES), BF16),
+            pltpu.VMEM((n, 2, LOCAL, tokens, LANES), BF16),
+            pltpu.VMEM((PAIRS, 2, GROUP, tokens, LANES), BF16),
+            pltpu.VMEM((2, GROUP, tokens, LANES), F32),
+            pltpu.VMEM((PAIRS, 2, GROUP + 1, tokens, LANES), BF16),
+            pltpu.VMEM((n, 2, GROUP + 1, tokens, LANES), BF16),
+            pltpu.VMEM((3, 2, GROUP, tokens, LANES), F32),
             pltpu.VMEM((LANES, 2 * GROUP * LANES), BF16),
-            pltpu.VMEM((KV_HEADS, GROUP, tokens, LANES), BF16),
+            pltpu.VMEM((PAIRS, 2, GROUP, tokens, LANES), BF16),
             pltpu.VMEM((n, tokens, block_width), BF16),
             pltpu.VMEM((tokens, width), F32),
             pltpu.VMEM((n, tokens, cols), BF16),
             pltpu.VMEM((n, tokens, cols), BF16),
+            pltpu.VMEM((2, batches, GROUP * tokens, cache_keys.shape[1]), F32),
             pltpu.SemaphoreType.DMA((8,)),
-            pltpu.SemaphoreType.DMA((7,)),
+            pltpu.SemaphoreType.DMA((2,)),
             pltpu.SemaphoreType.DMA((RECEIVES,)),
         ],
         compiler_params=pltpu.CompilerParams(
-            collective_id=0, has_side_effects=True, vmem_limit_bytes=57 * 1024 * 1024
+            collective_id=0, has_side_effects=True, vmem_limit_bytes=62 * 1024 * 1024
         ),
     )(
         *(in_vmem(a) for a in (blocks, gains, misc)),

time: 49.1 us -> 47.1 us (0.959)
  Pallas kernels: 48.2 us -> 46.3 us
    pallas_call x1, Pallas kernels: 45.1 us -> 43 us  [body(): pl.pallas_call(functools.partial(layer_kernel, n), out_shape=(pltpu.VMEM(...]
where the time goes in v2:
time: 47.1 us; the launch traced here: 46.9 us
  Pallas kernels  46.3 us (98%)
  between operations  0.65 us (1%)
    pallas_call x1, Pallas kernels, body(): pl.pallas_call(functools.partial(layer_kernel, n), out_shape=(pltpu.VMEM(...  43 us
    pallas_call x1, Pallas kernels, body(): pl.pallas_call(functools.partial(gather_kernel, n), out_shape=(pltpu.VMEM...  2.57 us

profile of v2, /device:TPU:0, one launch (start us, length us, event | category | flops | bytes accessed | tf_op | source)
XLA Modules:
  0.0 46.9 jit_solution(3620969740486160162)
XLA Ops:
  0.6 2.6 %shard_map.140 = (bf16[16,8,384]{2,1,0:T(8,128)(2,1)S(1)}, f32[16,8,320]{2,1,0:T(8,128)S(1)}, f32[3,8,128]{2,1,0:T(8,128)S(1)}) custom-call(s32[2,4]{1,0:T(2,128)} %bitcast.5, s32[2]{0:T(128)} %lengths_hbm.1, bf16[5120]{0:T(1024)(128)(2,1)} %gain_one_hbm.1, bf16[5120]{0:T(1024)(128)(2,1)} %gain_two_hbm.1, bf16[4752,5120]{1,0:T(8,128)(2,1)} %table.1), custom_call_target="tpu_custom_call" | custom-call | tf_op jit(solution)/shard_map/pallas_call | solution.py:649
  3.2 43.0 %shard_map.141 = (bf16[4,2,5120]{2,1,0:T(2,128)(2,1)S(1)}, bf16[4,2,320]{2,1,0:T(2,128)(2,1)S(1)}) custom-call(bf16[16,8,384]{2,1,0:T(8,128)(2,1)S(1)} %get-tuple-element.7.blocks, f32[16,8,320]{2,1,0:T(8,128)S(1)} %get-tuple-element.8.gains, f32[3,8,128]{2,1,0:T(8,128)S(1)} %get-tuple-element.9.misc, f32[56,128]{1,0:T(8,128)} %bitcast.4, ...), custom_call_target="tpu_custom_call" | custom-call | tf_op jit(solution)/shard_map/pallas_call | solution.py:671
  46.3 0.7 %shard_map.142 = (bf16[4,2,5120]{2,1,0:T(2,128)(2,1)}, bf16[4,2,320]{2,1,0:T(2,128)(2,1)}) custom-call(bf16[4,2,5120]{2,1,0:T(2,128)(2,1)S(1)} %get-tuple-element.10.attended, bf16[4,2,320]{2,1,0:T(2,128)(2,1)S(1)} %get-tuple-element.11.layer), custom_call_target="tpu_custom_call" | custom-call | tf_op jit(solution)/shard_map/pallas_call | solution.py:725

commit v3 on v2

--- a/solution.py
+++ b/solution.py
@@ -84,17 +84,15 @@
     row = lax.broadcasted_iota(jnp.int32, (tokens, tokens * 8), 0)
     lane = lax.broadcasted_iota(jnp.int32, (tokens, tokens * 8), 1)
     target = jnp.full((tokens, tokens * 8), -1, jnp.int32)
-    copies = []
     for t in range(tokens):
         local = ids[t // steps, t % steps] - me * vocab_rows
         inside = (local >= 0) & (local < vocab_rows)
         local = jnp.clip(local, 0, vocab_rows - 1)
         base = local // 8
         copy = pltpu.make_async_copy(
-            table.at[pl.ds(pl.multiple_of(base * 8, 8), 8), :], rows.at[t], row_sem.at[t]
+            table.at[pl.ds(pl.multiple_of(base * 8, 8), 8), :], rows.at[t], row_sem
         )
         copy.start()
-        copies.append(copy)
         target = jnp.where(row == t, jnp.where(inside, t * 8 + local - base * 8, -1), target)
     one_hot = jnp.where(lane == target, 1.0, 0.0).astype(BF16)
 
@@ -115,8 +113,7 @@
     misc[0] = jnp.cos(angle)
     misc[1] = jnp.where(first, -sine, sine)
 
-    for copy in copies:
-        copy.wait()
+    pltpu.make_async_copy(rows, rows, row_sem).wait()
     found = rows[...].astype(F32).reshape(tokens * 8, width).astype(BF16)
     wide[...] = jnp.dot(one_hot, found, preferred_element_type=F32)
     square = jnp.sum(wide[...] * wide[...], axis=1, keepdims=True)
@@ -178,7 +175,7 @@
     block_width = blocks.shape[2]
     batches, local_len = keys.shape[0], keys.shape[1]
     steps = tokens // batches
-    cols, width = w_out.shape
+    cols, width = out_hbm.shape
     units = w_gate.shape[1]
     group_width = GROUP * HEAD_DIM
     scale = 1.0 / math.sqrt(HEAD_DIM)
@@ -196,11 +193,11 @@
         pltpu.make_async_copy(a, b, load_sem.at[i])
         for i, (a, b) in enumerate(
             (
-                (qkv_hbm, w_qkv),
+                (qkv_hbm, w_qkv.at[:, pl.ds(0, qkv_hbm.shape[1])]),
                 (bias_hbm, bias),
-                (keys_hbm, keys),
-                (values_hbm, values),
-                (out_hbm, w_out),
+                (keys_hbm, keys.at[:, :, pl.ds(0, keys_hbm.shape[2])]),
+                (values_hbm, values.at[:, :, pl.ds(0, values_hbm.shape[2])]),
+                (out_hbm, w_out.at[:, pl.ds(0, width)]),
                 (gate_hbm, w_gate),
                 (up_hbm, w_up),
                 (down_hbm, w_down),
@@ -208,15 +205,6 @@
         )
     ]
     barrier = pltpu.get_barrier_semaphore()
-
-    @pl.loop(1, n)
-    def _(d):
-        pl.semaphore_signal(
-            barrier, inc=1, device_id={"seq": lax.rem(me + d, n)}, device_id_type=MESH
-        )
-
-    for load in loads:
-        load.start()
 
     unrolled = n & (n - 1) == 0 and n <= 32
     staged = unrolled and n // 4 <= 4 and cols % 16 == 0 and (4 * cols) % LANES == 0
@@ -238,6 +226,14 @@
             @pl.loop(1, n)
             def _(d):
                 act(lax.rem(me + d, n))
+
+    each_peer(
+        lambda peer: pl.semaphore_signal(
+            barrier, inc=1, device_id={"seq": peer}, device_id_type=MESH
+        )
+    )
+    for load in loads:
+        load.start()
 
     def copy_to(step, source, target, slot, peer, arrival=0):
         return pltpu.make_async_remote_copy(
@@ -396,7 +392,7 @@
     exponent = scale / math.log(2.0)
     near = [2 * side + turn, 2 * side + 1 - turn]
     far = [2 * (1 - side) + turn, 2 * (1 - side) + 1 - turn]
-    order = [near[0], far[0], far[1], near[1]]
+    order = [near[0], near[1], far[1], far[0]]
     def pair_cols(c):
         return pl.ds(pl.multiple_of(c * 2 * HEAD_DIM, LANES), 2 * HEAD_DIM)
 
@@ -443,7 +439,7 @@
             part_out[c, p, GROUP] = stats.astype(BF16)
 
     found = {}
-    for block in ((0,), (1, 2), (3, 4)):
+    for block in ((0, 1), (2,), (3, 4)):
         for r in block:
             if r < PAIRS:
 
@@ -663,7 +659,7 @@
             pltpu.VMEM((tokens, 8, width), BF16),
             pltpu.VMEM((tokens, width), F32),
             pltpu.SemaphoreType.DMA((4,)),
-            pltpu.SemaphoreType.DMA((tokens,)),
+            pltpu.SemaphoreType.DMA,
         ],
         compiler_params=pltpu.CompilerParams(vmem_limit_bytes=60 * 1024 * 1024),
     )(*(in_hbm(a) for a in (token_ids.T, lengths, attn_gain, mlp_gain, embed_table)))
@@ -680,8 +676,16 @@
             pltpu.VMEM((joint_heads, HEAD_DIM), F32),
         ]
         + [
-            pltpu.VMEM(a.shape, a.dtype)
-            for a in (w_qkv, cache_keys, cache_values, w_out.T, w_gate, w_up, w_down)
+            pltpu.VMEM((*a.shape[:-1], a.shape[-1] + more), a.dtype)
+            for a, more in (
+                (w_qkv, 2 * LANES),
+                (cache_keys, 2 * LANES),
+                (cache_values, 2 * LANES),
+                (w_out.T, 2 * LANES),
+                (w_gate, 0),
+                (w_up, 0),
+                (w_down, 0),
+            )
         ]
         + [
             pltpu.VMEM((n, tokens, block_width), BF16),
@@ -704,7 +708,7 @@
             pltpu.SemaphoreType.DMA((RECEIVES,)),
         ],
         compiler_params=pltpu.CompilerParams(
-            collective_id=0, has_side_effects=True, vmem_limit_bytes=62 * 1024 * 1024
+            collective_id=0, has_side_effects=True, vmem_limit_bytes=63 * 1024 * 1024
         ),
     )(
         *(in_vmem(a) for a in (blocks, gains, misc)),

time: 47.1 us -> 46.6 us (0.989)
  Pallas kernels: 46.3 us -> 45.8 us
where the time goes in v3:
time: 46.6 us; the launch traced here: 46.5 us
  Pallas kernels  45.8 us (98%)
  between operations  0.65 us (1%)
    pallas_call x1, Pallas kernels, body(): pl.pallas_call(functools.partial(layer_kernel, n), out_shape=(pltpu.VMEM(...  42.7 us
    pallas_call x1, Pallas kernels, body(): pl.pallas_call(functools.partial(gather_kernel, n), out_shape=(pltpu.VMEM...  2.44 us

profile of v3, /device:TPU:0, one launch (start us, length us, event | category | flops | bytes accessed | tf_op | source)
XLA Modules:
  0.0 46.5 jit_solution(9698382732956158854)
XLA Ops:
  0.6 2.4 %shard_map.140 = (bf16[16,8,384]{2,1,0:T(8,128)(2,1)S(1)}, f32[16,8,320]{2,1,0:T(8,128)S(1)}, f32[3,8,128]{2,1,0:T(8,128)S(1)}) custom-call(s32[2,4]{1,0:T(2,128)} %bitcast.5, s32[2]{0:T(128)} %lengths_hbm.1, bf16[5120]{0:T(1024)(128)(2,1)} %gain_one_hbm.1, bf16[5120]{0:T(1024)(128)(2,1)} %gain_two_hbm.1, bf16[4752,5120]{1,0:T(8,128)(2,1)} %table.1), custom_call_target="tpu_custom_call" | custom-call | tf_op jit(solution)/shard_map/pallas_call | solution.py:645
  3.1 42.7 %shard_map.141 = (bf16[4,2,5120]{2,1,0:T(2,128)(2,1)S(1)}, bf16[4,2,320]{2,1,0:T(2,128)(2,1)S(1)}) custom-call(bf16[16,8,384]{2,1,0:T(8,128)(2,1)S(1)} %get-tuple-element.7.blocks, f32[16,8,320]{2,1,0:T(8,128)S(1)} %get-tuple-element.8.gains, f32[3,8,128]{2,1,0:T(8,128)S(1)} %get-tuple-element.9.misc, f32[56,128]{1,0:T(8,128)} %bitcast.4, ...), custom_call_target="tpu_custom_call" | custom-call | tf_op jit(solution)/shard_map/pallas_call | solution.py:667
  45.8 0.7 %shard_map.142 = (bf16[4,2,5120]{2,1,0:T(2,128)(2,1)}, bf16[4,2,320]{2,1,0:T(2,128)(2,1)}) custom-call(bf16[4,2,5120]{2,1,0:T(2,128)(2,1)S(1)} %get-tuple-element.10.attended, bf16[4,2,320]{2,1,0:T(2,128)(2,1)S(1)} %get-tuple-element.11.layer), custom_call_target="tpu_custom_call" | custom-call | tf_op jit(solution)/shard_map/pallas_call | solution.py:729
